TPU v7x, 32 devices: a whole 2x2x4 slice. The times are simulated.
32 devices in a mesh: dp: 8 (over y, x, core), expert: 4 (over z).
Axes of the slice: x: 2, y: 2, z: 4, core: 2. Of those that a mesh axis runs over, the one named last changes fastest.
Arguments:
- tokens: bfloat16 [4096, 2048], P(('dp', 'expert')), may hold values from -6 to 6
- routes: int32 [4096, 2], P(('dp', 'expert')), may hold values from 0 to 3, as said below
- grad_hidden: bfloat16 [4096, 2, 768], P(('dp', 'expert')), may hold values from -1.1953125 to 1.1953125
- w_gate: bfloat16 [4, 2048, 768], P('expert'), may hold values from -0.125 to 0.125
- w_up: bfloat16 [4, 2048, 768], P('expert'), may hold values from -0.125 to 0.125
Outputs:
- grad_tokens: bfloat16 [4096, 2048], P(('dp', 'expert'))
- grad_gate: float32 [4, 2048, 768], P('expert', 'dp')
- grad_up: float32 [4, 2048, 768], P('expert', 'dp')
Inputs may be any that keep to these rules, and one draw needn't show every extreme that they name: `routes`: each row names 2 different experts. In each data group 2 experts are hot, the same for all rows of the group: in the rows of one device each hot expert of its group is named more often than every other expert and at most 73 times, every other expert at most 64 times. In the rows of every device some expert is named exactly 64 times; in the rows of some device a hot expert is named exactly 73 times. Every expert is hot in some data group. The indices of a group's two hot experts never differ by 2.
All inputs are finite; a program needn't handle non-finite values.
Results may differ from a plain program's by a relative error of at most 0.012.
Values may be sent and summed in bfloat16 or wider, within the bound.
A program may use at most 128 MiB of HBM per device.

v0:
```python
import functools

import jax
import jax.numpy as jnp
from jax import lax
from jax.experimental import pallas as pl
from jax.experimental.pallas import tpu as pltpu
from jax.sharding import PartitionSpec as P

MESH = pl.DeviceIdType.MESH
BF = jnp.bfloat16
F32 = jnp.float32


def dot(a, b, da, db):
    return lax.dot_general(a, b, (((da,), (db,)), ((), ())), preferred_element_type=F32)


def rs_plan(bits):
    orders = (tuple(range(bits)), (0,) + tuple(range(bits - 1, 0, -1)))
    index = {}
    for which, order in enumerate(orders):
        done = 1
        for bit in order[1:]:
            flag = 1 << bit
            for mask in range(1 << bits):
                if mask & done or mask & flag:
                    continue
                index[which, bit, mask] = len(index)
            done |= flag
    return orders, index


def kernel(
    groups, ways, cap, tok_ref, rt_ref, gh0_ref, gh1_ref, wg_hbm, wu_hbm,
    out_tok, out_gate, out_up,
    wg, wu, pick, send, rows, delta, back, ret, core_send, core_recv, hop_send, hop_recv, acc,
    w_sem, z_ssem, z_rsem, b_ssem, b_rsem, c_ssem, c_rsem, h_ssem, h_rsem,
):
    features = tok_ref.shape[1]
    toks = tok_ref.shape[0]
    hidden = gh0_ref.shape[1]
    block = features // ways
    bits = ways.bit_length() - 1
    orders, index = rs_plan(bits)
    me = lax.axis_index("expert")
    dp = lax.axis_index("dp")
    my_bits = [lax.rem(dp // (1 << b), 2) for b in range(bits)]

    def peer_dp(mask):
        total = 0
        for b in range(bits):
            bit = 1 - my_bits[b] if mask >> b & 1 else my_bits[b]
            total = total + bit * (1 << b)
        return total

    load_g = pltpu.make_async_copy(wg_hbm, wg, w_sem.at[0])
    load_u = pltpu.make_async_copy(wu_hbm, wu, w_sem.at[1])
    load_g.start()
    load_u.start()

    barrier = pltpu.get_barrier_semaphore()
    for off in range(1, groups):
        pl.semaphore_signal(
            barrier, inc=1, device_id={"expert": lax.rem(me + off, groups)}, device_id_type=MESH
        )
    for b in range(bits):
        pl.semaphore_signal(
            barrier, inc=1, device_id={"dp": peer_dp(1 << b)}, device_id_type=MESH
        )

    r0 = rt_ref[0:1, :]
    r1 = rt_ref[1:2, :]
    wide = max(groups, 8)
    ids = lax.broadcasted_iota(jnp.int32, (wide, toks), 0)
    is0 = (ids == r0).astype(F32)
    is1 = (ids == r1).astype(F32)
    before = (
        lax.broadcasted_iota(jnp.int32, (toks, toks), 0)
        < lax.broadcasted_iota(jnp.int32, (toks, toks), 1)
    ).astype(F32).astype(BF)
    earlier = dot((is0 + is1).astype(BF), before, 1, 0)
    pos0 = r0.astype(F32) * cap + jnp.sum(is0 * earlier, axis=0, keepdims=True)
    pos1 = r1.astype(F32) * cap + jnp.sum(is1 * earlier, axis=0, keepdims=True)
    slot = lax.broadcasted_iota(jnp.int32, (groups * cap, toks), 0).astype(F32)
    m0 = (slot == pos0).astype(F32)
    m1 = (slot == pos1).astype(F32)
    pick[...] = (m0 + m1).astype(BF)
    send[:, features:] = (
        dot(m0.astype(BF), gh0_ref[...], 1, 0) + dot(m1.astype(BF), gh1_ref[...], 1, 0)
    ).astype(BF)
    step = 512
    for c in range(0, features, step):
        send[:, c : c + step] = dot(pick[...], tok_ref[:, c : c + step], 1, 0).astype(BF)

    pl.semaphore_wait(barrier, groups - 1 + bits)

    def span(i):
        return pl.ds(pl.multiple_of(i * cap, cap), cap)

    def exchange(src, dst, ssem, rsem):
        sends, recvs = [], []
        for off in range(1, groups):
            to = lax.rem(me + off, groups)
            frm = lax.rem(me + groups - off, groups)
            sends.append(pltpu.make_async_remote_copy(
                src_ref=src.at[span(to)], dst_ref=dst.at[span(me)],
                send_sem=ssem.at[off], recv_sem=rsem.at[off],
                device_id={"expert": to}, device_id_type=MESH))
            recvs.append(pltpu.make_async_remote_copy(
                src_ref=src.at[span(frm)], dst_ref=dst.at[span(frm)],
                send_sem=ssem.at[off], recv_sem=rsem.at[off],
                device_id={"expert": frm}, device_id_type=MESH))
        for copy in sends:
            copy.start()
        return sends, recvs

    out_sends, out_recvs = exchange(send, rows, z_ssem, z_rsem)
    rows[span(me), :] = send[span(me), :]
    load_g.wait()
    load_u.wait()
    for copy in out_recvs:
        copy.wait_recv()

    tile = 256

    def forward(f, carry):
        cols = pl.ds(pl.multiple_of(f * tile, tile), tile)
        ucols = pl.ds(pl.multiple_of(f * tile + hidden, tile), tile)
        dcols = pl.ds(pl.multiple_of(f * tile + features, tile), tile)
        x = rows[:, 0:features]
        gate = dot(x, wg[:, cols], 1, 0)
        up = dot(x, wu[:, cols], 1, 0)
        sig = jax.nn.sigmoid(gate)
        grad = rows[:, dcols].astype(F32)
        delta[:, cols] = (grad * up * sig * (1.0 + gate * (1.0 - sig))).astype(BF)
        delta[:, ucols] = (grad * gate * sig).astype(BF)
        return carry

    lax.fori_loop(0, hidden // tile, forward, 0)

    def weight_block(mask):
        start = pl.multiple_of(peer_dp(mask) * block, block)
        return dot(rows[:, pl.ds(start, block)], delta[...], 0, 0)

    core_sends = {}
    for mask in range(ways - 1, 0, -2):
        place = mask >> 1
        core_send[place] = weight_block(mask).astype(BF)
        copy = pltpu.make_async_remote_copy(
            src_ref=core_send.at[place], dst_ref=core_recv.at[place],
            send_sem=c_ssem.at[place], recv_sem=c_rsem.at[place],
            device_id={"dp": peer_dp(1)}, device_id_type=MESH)
        copy.start()
        core_sends[place] = copy

    def backward(d, carry):
        cols = pl.ds(pl.multiple_of(d * tile, tile), tile)
        back[:, cols] = (
            dot(delta[:, 0:hidden], wg[cols, :], 1, 1)
            + dot(delta[:, hidden:], wu[cols, :], 1, 1)
        ).astype(BF)
        return carry

    lax.fori_loop(0, features // tile, backward, 0)
    back_sends, back_recvs = exchange(back, ret, b_ssem, b_rsem)
    ret[span(me), :] = back[span(me), :]

    hop_sends = []

    def hop(which, bit, mask, value):
        at = index[which, bit, mask ^ (1 << bit)]
        hop_send[at] = value.astype(BF)
        copy = pltpu.make_async_remote_copy(
            src_ref=hop_send.at[at], dst_ref=hop_recv.at[at],
            send_sem=h_ssem.at[at], recv_sem=h_rsem.at[at],
            device_id={"dp": peer_dp(1 << bit)}, device_id_type=MESH)
        copy.start()
        hop_sends.append(copy)

    def arrived(which, bit, mask):
        at = index[which, bit, mask]
        pltpu.make_async_remote_copy(
            src_ref=hop_send.at[at], dst_ref=hop_recv.at[at],
            send_sem=h_ssem.at[at], recv_sem=h_rsem.at[at],
            device_id={"dp": peer_dp(1 << bit)}, device_id_type=MESH).wait_recv()
        return hop_recv[at].astype(F32)

    for mask in range(ways - 2, -1, -2):
        place = mask >> 1
        core_sends[place].wait_recv()
        total = weight_block(mask) + core_recv[place].astype(F32)
        for which in range(2):
            part = total[:, which * hidden : (which + 1) * hidden]
            bit = orders[which][1]
            if mask >> bit & 1:
                hop(which, bit, mask, part)
            else:
                acc[which, place] = part

    for level in range(2, bits):
        for mask in range(ways - 2, -1, -2):
            for which in range(2):
                order = orders[which]
                fixed = sum(1 << b for b in order[:level])
                if mask & fixed:
                    continue
                value = acc[which, mask >> 1] + arrived(which, order[level - 1], mask)
                if mask >> order[level] & 1:
                    hop(which, order[level], mask, value)
                else:
                    acc[which, mask >> 1] = value

    for copy in back_recvs:
        copy.wait_recv()
    for c in range(0, features, step):
        out_tok[:, c : c + step] = dot(pick[...], ret[:, c : c + step], 0, 0).astype(BF)
    out_gate[...] = acc[0, 0] + arrived(0, orders[0][-1], 0)
    out_up[...] = acc[1, 0] + arrived(1, orders[1][-1], 0)

    for copy in out_sends + back_sends + list(core_sends.values()) + hop_sends:
        copy.wait_send()


def per_device(tokens, routes, grad_hidden, w_gate, w_up):
    tok_rows, features = tokens.shape
    per_token = routes.shape[1]
    hidden = w_gate.shape[2]
    groups = lax.axis_size("expert")
    ways = lax.axis_size("dp")
    pair_count = tok_rows * per_token
    cold_most = pair_count // groups
    cold_floor = cold_most - 2 - cold_most // 8
    hot_total = pair_count - (groups - 3) * cold_floor - cold_most
    hot_most = (hot_total + 1) // 2 + min((hot_total - 2 * cold_most - 2) // 2, cold_most // 4)
    cap = (max(hot_most, cold_most) + 15) // 16 * 16
    slots = groups * cap
    block = features // ways
    bits = ways.bit_length() - 1
    hops = len(rs_plan(bits)[1])
    half = ways // 2
    vmem = pl.BlockSpec(memory_space=pltpu.VMEM)
    hbm = pl.BlockSpec(memory_space=pl.ANY)
    dma = pltpu.SemaphoreType.DMA
    tok_grad, gate_grad, up_grad = pl.pallas_call(
        functools.partial(kernel, groups, ways, cap),
        out_shape=(
            jax.ShapeDtypeStruct((tok_rows, features), BF),
            jax.ShapeDtypeStruct((block, hidden), F32),
            jax.ShapeDtypeStruct((block, hidden), F32),
        ),
        in_specs=[vmem, vmem, vmem, vmem, hbm, hbm],
        out_specs=(vmem, vmem, vmem),
        scratch_shapes=[
            pltpu.VMEM((features, hidden), BF),
            pltpu.VMEM((features, hidden), BF),
            pltpu.VMEM((slots, tok_rows), BF),
            pltpu.VMEM((slots, features + hidden), BF),
            pltpu.VMEM((slots, features + hidden), BF),
            pltpu.VMEM((slots, 2 * hidden), BF),
            pltpu.VMEM((slots, features), BF),
            pltpu.VMEM((slots, features), BF),
            pltpu.VMEM((half, block, 2 * hidden), BF),
            pltpu.VMEM((half, block, 2 * hidden), BF),
            pltpu.VMEM((hops, block, hidden), BF),
            pltpu.VMEM((hops, block, hidden), BF),
            pltpu.VMEM((2, half, block, hidden), F32),
            dma((2,)),
            dma((groups,)),
            dma((groups,)),
            dma((groups,)),
            dma((groups,)),
            dma((half,)),
            dma((half,)),
            dma((hops,)),
            dma((hops,)),
        ],
        compiler_params=pltpu.CompilerParams(collective_id=0, has_side_effects=True),
    )(tokens, routes.T, grad_hidden[:, 0], grad_hidden[:, 1], w_gate[0], w_up[0])
    return tok_grad, gate_grad[None], up_grad[None]


def solution(mesh):
    placed = (
        P(("dp", "expert"), None),
        P(("dp", "expert"), None),
        P(("dp", "expert"), None, None),
        P("expert", None, None),
        P("expert", None, None),
    )
    return jax.shard_map(
        per_device,
        mesh=mesh,
        in_specs=placed,
        out_specs=(P(("dp", "expert"), None), P("expert", "dp", None), P("expert", "dp", None)),
        check_vma=False,
    )
```

profile of v0, /device:TPU:8, one launch (start us, length us, event | category | flops | bytes accessed | tf_op | source)
XLA Modules:
  0.0 89.4 jit_solution(14247878089507294373)
XLA Ops:
  0.6 1.8 %fusion = (bf16[128,1,768]{2,1,0:T(2,128)(2,1)S(1)}, bf16[128,1,768]{2,1,0:T(2,128)(2,1)S(1)}) fusion(bf16[128,2,768]{2,1,0:T(2,128)(2,1)} %param.7), kind=kLoop, calls=%fused_computation.2 | loop fusion | bytes 786432 | tf_op jit(solution)/shard_map/slice | solution.py:279
  2.4 0.8 copy_bitcast_fusion
  3.2 81.3 %shard_map.76 = (bf16[128,2048]{1,0:T(8,128)(2,1)}, f32[256,768]{1,0:T(8,128)}, f32[256,768]{1,0:T(8,128)}) custom-call(bf16[128,2048]{1,0:T(8,128)(2,1)} %tok_ref.1, s32[2,128]{1,0:T(2,128)} %bitcast.13, bf16[128,768]{1,0:T(8,128)(2,1)} %get-tuple-element.12.gh0_ref, bf16[128,768]{1,0:T(8,128)(2,1)} %get-tuple-element.11.gh1_ref, ...), custom_call_target="tpu_custom_call" | custom-call | tf_op jit(solution)/shard_map/pallas_call | solution.py:245
  84.5 0.0 copy-start
  84.5 2.0 %copy.17 = bf16[128,2048]{1,0:T(8,128)(2,1)} copy(bf16[128,2048]{1,0:T(8,128)(2,1)} %get-tuple-element.16) | data formatting | bytes 1048576
  86.5 2.1 %copy.18 = f32[1,256,768]{2,1,0:T(8,128)} copy(f32[1,256,768]{2,1,0:T(8,128)} %bitcast.12) | data formatting | bytes 1572864
  88.5 0.0 copy-done
  88.5 0.9 copy.19
Async XLA Ops:
  84.5 4.0 %copy-start = (f32[256,768]{1,0:T(8,128)S(1)}, f32[256,768]{1,0:T(8,128)}, u32[]{:S(2)}) copy-start(f32[256,768]{1,0:T(8,128)} %get-tuple-element.8) | copy-start | bytes 2359300
where the time goes:
time: 90 us; the launch traced here: 89.4 us
  Pallas kernels  81.3 us (90%)
  local copies, waits for them, and re-layouts  7.48 us (8%)
    pallas_call x1, Pallas kernels, per_device(): pl.pallas_call(functools.partial(kernel, groups, ways, cap), out_shape=(j...  81.3 us
    unnamed x5, local copies, waits for them, and re-layouts  4.9 us

commit v1 on v0

--- a/solution.py
+++ b/solution.py
@@ -222,6 +222,238 @@
         copy.wait_send()
 
 
+def gather_plan(bits):
+    if bits > 2:
+        orders = (tuple(range(1, bits)) + (0,), tuple(range(bits - 1, 0, -1)) + (0,))
+    else:
+        orders = (tuple(range(bits - 1, -1, -1)),) * 2
+    via = {}
+    for part, order in enumerate(orders):
+        for mask in range(1, 1 << bits):
+            via[mask, part] = [b for b in order if mask >> b & 1][-1]
+    masks = sorted(range(1, 1 << bits), key=lambda mask: (bin(mask).count("1"), mask))
+    return masks, via
+
+
+def gather_kernel(
+    groups, ways, cap, tok_ref, rt_ref, gh0_ref, gh1_ref, wg_hbm, wu_hbm,
+    out_tok, out_gate, out_up,
+    wg, wu, pick, pick0, pick1, sx, sd, rx, rd, dg, xg, sback, ret, acc,
+    w_sem, x_ss, x_rs, d_ss, d_rs, b_ss, b_rs, g_ss, g_rs, c_ss, c_rs,
+):
+    features = tok_ref.shape[1]
+    toks = tok_ref.shape[0]
+    hidden = gh0_ref.shape[1]
+    block = features // ways
+    bits = ways.bit_length() - 1
+    masks, via = gather_plan(bits)
+    me = lax.axis_index("expert")
+    dp = lax.axis_index("dp")
+
+    def flip(value, mask, count):
+        total = 0
+        for b in range(count):
+            bit = lax.rem(value // (1 << b), 2)
+            if mask >> b & 1:
+                bit = 1 - bit
+            total = total + bit * (1 << b)
+        return total
+
+    partner = [flip(me, k, groups.bit_length() - 1) for k in range(groups)]
+    peer = [flip(dp, m, bits) for m in range(ways)]
+
+    load_g = pltpu.make_async_copy(wg_hbm, wg, w_sem.at[0])
+    load_u = pltpu.make_async_copy(wu_hbm, wu, w_sem.at[1])
+    load_g.start()
+    load_u.start()
+
+    barrier = pltpu.get_barrier_semaphore()
+    for k in range(1, groups):
+        pl.semaphore_signal(barrier, inc=1, device_id={"expert": partner[k]}, device_id_type=MESH)
+    for m in range(1, ways):
+        pl.semaphore_signal(barrier, inc=1, device_id={"dp": peer[m]}, device_id_type=MESH)
+
+    r0 = rt_ref[0:1, :]
+    r1 = rt_ref[1:2, :]
+    wide = max(groups, 8)
+    ids = lax.broadcasted_iota(jnp.int32, (wide, toks), 0)
+    is0 = (ids == r0).astype(F32)
+    is1 = (ids == r1).astype(F32)
+    before = (
+        lax.broadcasted_iota(jnp.int32, (toks, toks), 0)
+        < lax.broadcasted_iota(jnp.int32, (toks, toks), 1)
+    ).astype(F32).astype(BF)
+    earlier = dot((is0 + is1).astype(BF), before, 1, 0)
+    pos0 = r0.astype(F32) * cap + jnp.sum(is0 * earlier, axis=0, keepdims=True)
+    pos1 = r1.astype(F32) * cap + jnp.sum(is1 * earlier, axis=0, keepdims=True)
+    slot = lax.broadcasted_iota(jnp.int32, (groups * cap, toks), 0).astype(F32)
+    m0 = (slot == pos0).astype(F32)
+    m1 = (slot == pos1).astype(F32)
+    pick0[...] = m0.astype(BF)
+    pick1[...] = m1.astype(BF)
+    pick[...] = (m0 + m1).astype(BF)
+
+    def span(i):
+        return pl.ds(pl.multiple_of(i * cap, cap), cap)
+
+    def to_expert(src, dst, ssem, rsem, k):
+        return pltpu.make_async_remote_copy(
+            src_ref=src.at[k], dst_ref=dst.at[k], send_sem=ssem.at[k], recv_sem=rsem.at[k],
+            device_id={"expert": partner[k]}, device_id_type=MESH)
+
+    pending = []
+    x_copy, d_copy, b_copy = {}, {}, {}
+    step = 512
+    greeted = False
+    for k in list(range(1, groups)) + [0]:
+        rows_x = sx if k else rx
+        rows_d = sd if k else rd
+        for c in range(0, features, step):
+            rows_x[k, :, c : c + step] = dot(
+                pick[span(partner[k]), :], tok_ref[:, c : c + step], 1, 0).astype(BF)
+        if not greeted:
+            pl.semaphore_wait(barrier, groups - 1 + ways - 1)
+            greeted = True
+        if k:
+            x_copy[k] = to_expert(sx, rx, x_ss, x_rs, k)
+            x_copy[k].start()
+        rows_d[k] = (
+            dot(pick0[span(partner[k]), :], gh0_ref[...], 1, 0)
+            + dot(pick1[span(partner[k]), :], gh1_ref[...], 1, 0)
+        ).astype(BF)
+        if k:
+            d_copy[k] = to_expert(sd, rd, d_ss, d_rs, k)
+            d_copy[k].start()
+            pending += [x_copy[k], d_copy[k]]
+
+    tile = 256
+
+    def place(mask):
+        return pl.ds(mask * cap, cap)
+
+    def part_cols(part):
+        return pl.ds(part * hidden, hidden)
+
+    def delta_copy(k, mask, part):
+        bit = via[mask, part]
+        return pltpu.make_async_remote_copy(
+            src_ref=dg.at[k, place(mask ^ (1 << bit)), part_cols(part)],
+            dst_ref=dg.at[k, place(mask), part_cols(part)],
+            send_sem=c_ss.at[k, mask, part], recv_sem=c_rs.at[k, mask, part],
+            device_id={"dp": peer[1 << bit]}, device_id_type=MESH)
+
+    def rows_copy(k, mask):
+        start = pl.multiple_of(peer[mask] * block, block)
+        return pltpu.make_async_remote_copy(
+            src_ref=rx.at[k, :, pl.ds(start, block)],
+            dst_ref=xg.at[k, place(mask)],
+            send_sem=g_ss.at[k, mask], recv_sem=g_rs.at[k, mask],
+            device_id={"dp": peer[mask]}, device_id_type=MESH)
+
+    waited = set()
+
+    def arrive(k, mask, part):
+        if mask and (k, mask, part) not in waited:
+            waited.add((k, mask, part))
+            delta_copy(k, mask, part).wait_recv()
+
+    def pass_on(k, level):
+        for mask in masks:
+            if bin(mask).count("1") != level:
+                continue
+            for part in range(2):
+                arrive(k, mask ^ (1 << via[mask, part]), part)
+                copy = delta_copy(k, mask, part)
+                copy.start()
+                pending.append(copy)
+
+    def compute(k):
+        if k:
+            x_copy[k].wait_recv()
+        for mask in masks[::-1]:
+            copy = rows_copy(k, mask)
+            copy.start()
+            pending.append(copy)
+        if k == 0:
+            load_g.wait()
+            load_u.wait()
+        else:
+            d_copy[k].wait_recv()
+
+        def forward(f, carry):
+            cols = pl.ds(pl.multiple_of(f * tile, tile), tile)
+            ucols = pl.ds(pl.multiple_of(f * tile + hidden, tile), tile)
+            x = rx[k]
+            gate = dot(x, wg[:, cols], 1, 0)
+            up = dot(x, wu[:, cols], 1, 0)
+            sig = jax.nn.sigmoid(gate)
+            grad = rd[k, :, cols].astype(F32)
+            dg[k, 0:cap, cols] = (grad * up * sig * (1.0 + gate * (1.0 - sig))).astype(BF)
+            dg[k, 0:cap, ucols] = (grad * gate * sig).astype(BF)
+            return carry
+
+        lax.fori_loop(0, hidden // tile, forward, 0)
+        pass_on(k, 1)
+        held = sback if k else ret
+
+        def backward(d, carry):
+            cols = pl.ds(pl.multiple_of(d * tile, tile), tile)
+            held[k, :, cols] = (
+                dot(dg[k, 0:cap, 0:hidden], wg[cols, :], 1, 1)
+                + dot(dg[k, 0:cap, hidden:], wu[cols, :], 1, 1)
+            ).astype(BF)
+            return carry
+
+        lax.fori_loop(0, features // tile, backward, 0)
+        if k:
+            b_copy[k] = to_expert(sback, ret, b_ss, b_rs, k)
+            b_copy[k].start()
+            pending.append(b_copy[k])
+        start = pl.multiple_of(dp * block, block)
+        xg[k, 0:cap, :] = rx[k, :, pl.ds(start, block)]
+
+    def weight(k):
+        for mask in masks:
+            rows_copy(k, mask).wait_recv()
+            for part in range(2):
+                arrive(k, mask, part)
+        for part in range(2):
+            value = dot(xg[k], dg[k, :, part * hidden : (part + 1) * hidden], 0, 0)
+            if k == 0:
+                acc[part] = value
+            elif k < groups - 1:
+                acc[part] += value
+            else:
+                (out_gate, out_up)[part][...] = acc[part] + value
+
+    for k in range(groups):
+        compute(k)
+        for level in range(bits, 2, -1):
+            if k - level + 2 >= 0:
+                pass_on(k - level + 2, level)
+        pass_on(k, 2)
+        if k >= bits:
+            weight(k - bits)
+    for k in range(groups, groups + bits - 2):
+        for level in range(bits, 2, -1):
+            if 0 <= k - level + 2 < groups:
+                pass_on(k - level + 2, level)
+    for k in range(max(groups - bits, 0), groups - 1):
+        weight(k)
+
+    for k in range(1, groups):
+        b_copy[k].wait_recv()
+    for c in range(0, features, step):
+        total = dot(pick[span(partner[0]), :], ret[0, :, c : c + step], 0, 0)
+        for k in range(1, groups):
+            total = total + dot(pick[span(partner[k]), :], ret[k, :, c : c + step], 0, 0)
+        out_tok[:, c : c + step] = total.astype(BF)
+    weight(groups - 1)
+
+    for copy in pending:
+        copy.wait_send()
+
+
 def per_device(tokens, routes, grad_hidden, w_gate, w_up):
     tok_rows, features = tokens.shape
     per_token = routes.shape[1]
@@ -242,6 +474,50 @@
     vmem = pl.BlockSpec(memory_space=pltpu.VMEM)
     hbm = pl.BlockSpec(memory_space=pl.ANY)
     dma = pltpu.SemaphoreType.DMA
+    held = 2 * (
+        2 * features * hidden + 3 * slots * tok_rows + 2 * slots * (2 * features + hidden)
+        + ways * slots * (2 * hidden + block) + 2 * tok_rows * (features + hidden)
+    ) + 4 * 4 * block * hidden
+    if groups & (groups - 1) == 0 and bits >= 2 and held < 3 * (1 << 24):
+        tok_grad, gate_grad, up_grad = pl.pallas_call(
+            functools.partial(gather_kernel, groups, ways, cap),
+            out_shape=(
+                jax.ShapeDtypeStruct((tok_rows, features), BF),
+                jax.ShapeDtypeStruct((block, hidden), F32),
+                jax.ShapeDtypeStruct((block, hidden), F32),
+            ),
+            in_specs=[vmem, vmem, vmem, vmem, hbm, hbm],
+            out_specs=(vmem, vmem, vmem),
+            scratch_shapes=[
+                pltpu.VMEM((features, hidden), BF),
+                pltpu.VMEM((features, hidden), BF),
+                pltpu.VMEM((slots, tok_rows), BF),
+                pltpu.VMEM((slots, tok_rows), BF),
+                pltpu.VMEM((slots, tok_rows), BF),
+                pltpu.VMEM((groups, cap, features), BF),
+                pltpu.VMEM((groups, cap, hidden), BF),
+                pltpu.VMEM((groups, cap, features), BF),
+                pltpu.VMEM((groups, cap, hidden), BF),
+                pltpu.VMEM((groups, ways * cap, 2 * hidden), BF),
+                pltpu.VMEM((groups, ways * cap, block), BF),
+                pltpu.VMEM((groups, cap, features), BF),
+                pltpu.VMEM((groups, cap, features), BF),
+                pltpu.VMEM((2, block, hidden), F32),
+                dma((2,)),
+                dma((groups,)),
+                dma((groups,)),
+                dma((groups,)),
+                dma((groups,)),
+                dma((groups,)),
+                dma((groups,)),
+                dma((groups, ways)),
+                dma((groups, ways)),
+                dma((groups, ways, 2)),
+                dma((groups, ways, 2)),
+            ],
+            compiler_params=pltpu.CompilerParams(collective_id=0, has_side_effects=True),
+        )(tokens, routes.T, grad_hidden[:, 0], grad_hidden[:, 1], w_gate[0], w_up[0])
+        return tok_grad, gate_grad[None], up_grad[None]
     tok_grad, gate_grad, up_grad = pl.pallas_call(
         functools.partial(kernel, groups, ways, cap),
         out_shape=(

time: 90 us -> 86.7 us (0.963)
  Pallas kernels: 81.3 us -> 78.4 us
    pallas_call x1, Pallas kernels: 81.3 us -> 78.4 us  [per_device(): pl.pallas_call(functools.partial(gather_kernel, groups, ways, cap), out_s...]
where the time goes in v1:
time: 86.7 us; the launch traced here: 86.5 us
  Pallas kernels  78.4 us (90%)
  local copies, waits for them, and re-layouts  7.48 us (9%)
    pallas_call x1, Pallas kernels, per_device(): pl.pallas_call(functools.partial(gather_kernel, groups, ways, cap), out_s...  78.4 us
    unnamed x5, local copies, waits for them, and re-layouts  4.9 us
    slice x1, local copies, waits for them, and re-layouts, per_device(): grad_hidden[:, 1]  1.79 us

profile of v1, /device:TPU:8, one launch (start us, length us, event | category | flops | bytes accessed | tf_op | source)
XLA Modules:
  0.0 86.5 jit_solution(9775600946445560520)
XLA Ops:
  0.6 1.8 %fusion = (bf16[128,1,768]{2,1,0:T(2,128)(2,1)S(1)}, bf16[128,1,768]{2,1,0:T(2,128)(2,1)S(1)}) fusion(bf16[128,2,768]{2,1,0:T(2,128)(2,1)} %param.7), kind=kLoop, calls=%fused_computation.2 | loop fusion | bytes 786432 | tf_op jit(solution)/shard_map/slice | solution.py:519
  2.4 0.8 copy_bitcast_fusion
  3.2 78.4 %shard_map.76 = (bf16[128,2048]{1,0:T(8,128)(2,1)}, f32[256,768]{1,0:T(8,128)}, f32[256,768]{1,0:T(8,128)}) custom-call(bf16[128,2048]{1,0:T(8,128)(2,1)} %tok_ref.1, s32[2,128]{1,0:T(2,128)} %bitcast.13, bf16[128,768]{1,0:T(8,128)(2,1)} %get-tuple-element.12.gh0_ref, bf16[128,768]{1,0:T(8,128)(2,1)} %get-tuple-element.11.gh1_ref, ...), custom_call_target="tpu_custom_call" | custom-call | tf_op jit(solution)/shard_map/pallas_call | solution.py:482
  81.6 0.0 copy-start
  81.6 2.0 %copy.17 = bf16[128,2048]{1,0:T(8,128)(2,1)} copy(bf16[128,2048]{1,0:T(8,128)(2,1)} %get-tuple-element.16) | data formatting | bytes 1048576
  83.6 2.1 %copy.18 = f32[1,256,768]{2,1,0:T(8,128)} copy(f32[1,256,768]{2,1,0:T(8,128)} %bitcast.12) | data formatting | bytes 1572864
  85.6 0.0 copy-done
  85.6 0.9 %copy.19 = f32[1,256,768]{2,1,0:T(8,128)} copy(f32[1,256,768]{2,1,0:T(8,128)S(1)} %bitcast.11) | data formatting | bytes 1572864
Async XLA Ops:
  81.6 4.0 %copy-start = (f32[256,768]{1,0:T(8,128)S(1)}, f32[256,768]{1,0:T(8,128)}, u32[]{:S(2)}) copy-start(f32[256,768]{1,0:T(8,128)} %get-tuple-element.8) | copy-start | bytes 2359300

commit v2 on v1

--- a/solution.py
+++ b/solution.py
@@ -235,15 +235,44 @@
     return masks, via
 
 
+def fold_width(extra, width):
+    return width // 2 + (extra - 8) * 128
+
+
+def fold(extra, rows):
+    width = rows.shape[1]
+    parts = [jnp.concatenate([rows[0:8, : width // 2], rows[0:8, width // 2 :]], axis=0)]
+    sub = lax.broadcasted_iota(jnp.int32, (16, 128), 0)
+    for j in range(8, extra):
+        total = jnp.zeros((16, 128), F32)
+        for c in range(width // 128):
+            total = jnp.where(sub == c, rows[j : j + 1, c * 128 : (c + 1) * 128], total)
+        parts.append(total)
+    return jnp.concatenate([p.astype(BF) for p in parts], axis=1)
+
+
+def unfold(extra, folded, width):
+    rows = folded.astype(F32)
+    top = jnp.concatenate([rows[0:8, : width // 2], rows[8:16, : width // 2]], axis=1)
+    sub = lax.broadcasted_iota(jnp.int32, (8, width), 0)
+    low = jnp.zeros((8, width), F32)
+    for j in range(8, extra):
+        at = width // 2 + (j - 8) * 128
+        row = jnp.concatenate(
+            [rows[c : c + 1, at : at + 128] for c in range(width // 128)], axis=1)
+        low = jnp.where(sub == j - 8, row, low)
+    return jnp.concatenate([top, low], axis=0).astype(BF)
+
+
 def gather_kernel(
-    groups, ways, cap, tok_ref, rt_ref, gh0_ref, gh1_ref, wg_hbm, wu_hbm,
+    groups, ways, cap, base, extra, rt_hbm, tok_hbm, gh_hbm, wg_hbm, wu_hbm,
     out_tok, out_gate, out_up,
-    wg, wu, pick, pick0, pick1, sx, sd, rx, rd, dg, xg, sback, ret, acc,
-    w_sem, x_ss, x_rs, d_ss, d_rs, b_ss, b_rs, g_ss, g_rs, c_ss, c_rs,
+    rt_ref, tok_ref, gh_ref, wg, wu, pick, both, sides, sx, sd, so, rx, rd, ro, dg, xg, sback, sbo, ret, rbo, acc,
+    l_sem, x_ss, x_rs, d_ss, d_rs, o_ss, o_rs, b_ss, b_rs, e_ss, e_rs, g_ss, g_rs, c_ss, c_rs,
 ):
-    features = tok_ref.shape[1]
-    toks = tok_ref.shape[0]
-    hidden = gh0_ref.shape[1]
+    toks, features = tok_ref.shape
+    hidden = gh_ref.shape[2]
+    wide_x = fold_width(extra, features)
     block = features // ways
     bits = ways.bit_length() - 1
     masks, via = gather_plan(bits)
@@ -262,8 +291,14 @@
     partner = [flip(me, k, groups.bit_length() - 1) for k in range(groups)]
     peer = [flip(dp, m, bits) for m in range(ways)]
 
-    load_g = pltpu.make_async_copy(wg_hbm, wg, w_sem.at[0])
-    load_u = pltpu.make_async_copy(wu_hbm, wu, w_sem.at[1])
+    load_r = pltpu.make_async_copy(rt_hbm, rt_ref, l_sem.at[4])
+    load_r.start()
+    load_t = pltpu.make_async_copy(tok_hbm, tok_ref, l_sem.at[0])
+    load_d = pltpu.make_async_copy(gh_hbm, gh_ref, l_sem.at[1])
+    load_g = pltpu.make_async_copy(wg_hbm, wg, l_sem.at[2])
+    load_u = pltpu.make_async_copy(wu_hbm, wu, l_sem.at[3])
+    load_t.start()
+    load_d.start()
     load_g.start()
     load_u.start()
 
@@ -273,6 +308,7 @@
     for m in range(1, ways):
         pl.semaphore_signal(barrier, inc=1, device_id={"dp": peer[m]}, device_id_type=MESH)
 
+    load_r.wait()
     r0 = rt_ref[0:1, :]
     r1 = rt_ref[1:2, :]
     wide = max(groups, 8)
@@ -289,42 +325,58 @@
     slot = lax.broadcasted_iota(jnp.int32, (groups * cap, toks), 0).astype(F32)
     m0 = (slot == pos0).astype(F32)
     m1 = (slot == pos1).astype(F32)
-    pick0[...] = m0.astype(BF)
-    pick1[...] = m1.astype(BF)
     pick[...] = (m0 + m1).astype(BF)
-
-    def span(i):
-        return pl.ds(pl.multiple_of(i * cap, cap), cap)
+    both[:, 0:toks] = m0.astype(BF)
+    both[:, toks:] = m1.astype(BF)
+
+    def rows_of(k, start, count):
+        return pl.ds(pl.multiple_of(partner[k] * cap + start, 16), count)
 
     def to_expert(src, dst, ssem, rsem, k):
+        return pltpu.make_async_remote_copy(
+            src_ref=src.at[k, pl.ds(0, base)], dst_ref=dst.at[k, pl.ds(0, base)],
+            send_sem=ssem.at[k], recv_sem=rsem.at[k],
+            device_id={"expert": partner[k]}, device_id_type=MESH)
+
+    def rest_to_expert(src, dst, ssem, rsem, k):
         return pltpu.make_async_remote_copy(
             src_ref=src.at[k], dst_ref=dst.at[k], send_sem=ssem.at[k], recv_sem=rsem.at[k],
             device_id={"expert": partner[k]}, device_id_type=MESH)
 
     pending = []
-    x_copy, d_copy, b_copy = {}, {}, {}
+    x_copy, d_copy, o_copy, b_copy, e_copy = {}, {}, {}, {}, {}
     step = 512
+    sequence = [0, 1] + list(range(groups - 1, 1, -1))
+    load_t.wait()
     greeted = False
-    for k in list(range(1, groups)) + [0]:
-        rows_x = sx if k else rx
-        rows_d = sd if k else rd
+    for k in sequence[1:] + [0]:
+        dest, count = (sx, base) if k else (rx, cap)
         for c in range(0, features, step):
-            rows_x[k, :, c : c + step] = dot(
-                pick[span(partner[k]), :], tok_ref[:, c : c + step], 1, 0).astype(BF)
+            dest[k, 0:count, c : c + step] = dot(
+                pick[rows_of(k, 0, count), :], tok_ref[:, c : c + step], 1, 0).astype(BF)
         if not greeted:
-            pl.semaphore_wait(barrier, groups - 1 + ways - 1)
-            greeted = True
+            with jax.named_scope("p_barrier"):
+                pl.semaphore_wait(barrier, groups - 1 + ways - 1)
         if k:
             x_copy[k] = to_expert(sx, rx, x_ss, x_rs, k)
             x_copy[k].start()
-        rows_d[k] = (
-            dot(pick0[span(partner[k]), :], gh0_ref[...], 1, 0)
-            + dot(pick1[span(partner[k]), :], gh1_ref[...], 1, 0)
-        ).astype(BF)
+            pending.append(x_copy[k])
+        if not greeted:
+            greeted = True
+            load_d.wait()
+            sides[0:toks, :] = gh_ref[:, 0, :]
+            sides[toks:, :] = gh_ref[:, 1, :]
+        dest = sd if k else rd
+        dest[k, 0:count, :] = dot(both[rows_of(k, 0, count), :], sides[...], 1, 0).astype(BF)
         if k:
             d_copy[k] = to_expert(sd, rd, d_ss, d_rs, k)
             d_copy[k].start()
-            pending += [x_copy[k], d_copy[k]]
+            over = rows_of(k, base, cap - base)
+            so[k, :, 0:wide_x] = fold(extra, dot(pick[over, :], tok_ref[...], 1, 0))
+            so[k, :, wide_x:] = fold(extra, dot(both[over, :], sides[...], 1, 0))
+            o_copy[k] = rest_to_expert(so, ro, o_ss, o_rs, k)
+            o_copy[k].start()
+            pending += [d_copy[k], o_copy[k]]
 
     tile = 256
 
@@ -358,18 +410,23 @@
             delta_copy(k, mask, part).wait_recv()
 
     def pass_on(k, level):
-        for mask in masks:
-            if bin(mask).count("1") != level:
-                continue
-            for part in range(2):
-                arrive(k, mask ^ (1 << via[mask, part]), part)
-                copy = delta_copy(k, mask, part)
-                copy.start()
-                pending.append(copy)
+        steps = [(m, part) for part in range(2) for m in masks if bin(m).count("1") == level]
+        steps.sort(key=lambda step: (via[step] == 0, step[1] != step[0] // (ways // 2)))
+        for mask, part in steps:
+            arrive(k, mask ^ (1 << via[mask, part]), part)
+            copy = delta_copy(k, mask, part)
+            copy.start()
+            pending.append(copy)
 
     def compute(k):
         if k:
-            x_copy[k].wait_recv()
+            with jax.named_scope(f"p_x{k}"):
+                x_copy[k].wait_recv()
+            with jax.named_scope(f"p_d{k}"):
+                d_copy[k].wait_recv()
+                o_copy[k].wait_recv()
+            rx[k, base:cap, :] = unfold(extra, ro[k, :, 0:wide_x], features)
+            rd[k, base:cap, :] = unfold(extra, ro[k, :, wide_x:], hidden)
         for mask in masks[::-1]:
             copy = rows_copy(k, mask)
             copy.start()
@@ -377,8 +434,6 @@
         if k == 0:
             load_g.wait()
             load_u.wait()
-        else:
-            d_copy[k].wait_recv()
 
         def forward(f, carry):
             cols = pl.ds(pl.multiple_of(f * tile, tile), tile)
@@ -392,7 +447,8 @@
             dg[k, 0:cap, ucols] = (grad * gate * sig).astype(BF)
             return carry
 
-        lax.fori_loop(0, hidden // tile, forward, 0)
+        with jax.named_scope(f"p_fwd{k}"):
+            lax.fori_loop(0, hidden // tile, forward, 0)
         pass_on(k, 1)
         held = sback if k else ret
 
@@ -404,54 +460,76 @@
             ).astype(BF)
             return carry
 
-        lax.fori_loop(0, features // tile, backward, 0)
+        with jax.named_scope(f"p_back{k}"):
+            lax.fori_loop(0, features // tile, backward, 0)
         if k:
             b_copy[k] = to_expert(sback, ret, b_ss, b_rs, k)
             b_copy[k].start()
-            pending.append(b_copy[k])
+            sbo[k] = fold(extra, sback[k, base:cap, :].astype(F32))
+            e_copy[k] = rest_to_expert(sbo, rbo, e_ss, e_rs, k)
+            e_copy[k].start()
+            pending.extend([b_copy[k], e_copy[k]])
         start = pl.multiple_of(dp * block, block)
         xg[k, 0:cap, :] = rx[k, :, pl.ds(start, block)]
 
     def weight(k):
-        for mask in masks:
-            rows_copy(k, mask).wait_recv()
-            for part in range(2):
-                arrive(k, mask, part)
+        with jax.named_scope(f"p_got{k}"):
+            for mask in masks:
+                rows_copy(k, mask).wait_recv()
+                for part in range(2):
+                    arrive(k, mask, part)
         for part in range(2):
             value = dot(xg[k], dg[k, :, part * hidden : (part + 1) * hidden], 0, 0)
-            if k == 0:
+            if k == sequence[0]:
                 acc[part] = value
-            elif k < groups - 1:
+            elif k != sequence[-1]:
                 acc[part] += value
             else:
                 (out_gate, out_up)[part][...] = acc[part] + value
 
-    for k in range(groups):
-        compute(k)
-        for level in range(bits, 2, -1):
-            if k - level + 2 >= 0:
-                pass_on(k - level + 2, level)
-        pass_on(k, 2)
-        if k >= bits:
-            weight(k - bits)
-    for k in range(groups, groups + bits - 2):
-        for level in range(bits, 2, -1):
-            if 0 <= k - level + 2 < groups:
-                pass_on(k - level + 2, level)
-    for k in range(max(groups - bits, 0), groups - 1):
-        weight(k)
+    def hop(at, level):
+        if 0 <= at < groups:
+            with jax.named_scope(f"p_pass{sequence[at]}_{level}"):
+                pass_on(sequence[at], level)
+
+    for at in range(groups + bits):
+        if at < groups:
+            compute(sequence[at])
+        for level in range(2, bits + 1):
+            hop(at + 1 - level, level)
+        if bits <= at < groups + bits - 1:
+            weight(sequence[at - bits])
 
     for k in range(1, groups):
-        b_copy[k].wait_recv()
+        with jax.named_scope(f"p_ret{k}"):
+            b_copy[k].wait_recv()
+            e_copy[k].wait_recv()
+        ret[k, base:cap, :] = unfold(extra, rbo[k], features)
     for c in range(0, features, step):
-        total = dot(pick[span(partner[0]), :], ret[0, :, c : c + step], 0, 0)
+        total = dot(pick[rows_of(0, 0, cap), :], ret[0, :, c : c + step], 0, 0)
         for k in range(1, groups):
-            total = total + dot(pick[span(partner[k]), :], ret[k, :, c : c + step], 0, 0)
+            total = total + dot(pick[rows_of(k, 0, cap), :], ret[k, :, c : c + step], 0, 0)
         out_tok[:, c : c + step] = total.astype(BF)
-    weight(groups - 1)
-
-    for copy in pending:
-        copy.wait_send()
+    weight(sequence[-1])
+
+    with jax.named_scope("p_drain"):
+        for copy in pending:
+            copy.wait_send()
+
+
+def flush_kernel(tok, gate, up, out_tok, out_gate, out_up, sems):
+    copies = [
+        pltpu.make_async_copy(src, dst, sems.at[i])
+        for i, (src, dst) in enumerate(((tok, out_tok), (gate, out_gate), (up, out_up)))
+    ]
+    for copy in copies:
+        copy.start()
+    for copy in copies:
+        copy.wait()
+
+
+def pin(array):
+    return pltpu.with_memory_space_constraint(array, pltpu.HBM)
 
 
 def per_device(tokens, routes, grad_hidden, w_gate, w_up):
@@ -474,49 +552,60 @@
     vmem = pl.BlockSpec(memory_space=pltpu.VMEM)
     hbm = pl.BlockSpec(memory_space=pl.ANY)
     dma = pltpu.SemaphoreType.DMA
+    base = max(hot_most, cold_most) // 16 * 16
+    extra = max(hot_most, cold_most) - base
     held = 2 * (
-        2 * features * hidden + 3 * slots * tok_rows + 2 * slots * (2 * features + hidden)
-        + ways * slots * (2 * hidden + block) + 2 * tok_rows * (features + hidden)
+        2 * features * hidden + 3 * slots * tok_rows + 5 * slots * (features + hidden)
+        + ways * slots * (2 * hidden + block) + 2 * tok_rows * (features + 4 * hidden)
     ) + 4 * 4 * block * hidden
-    if groups & (groups - 1) == 0 and bits >= 2 and held < 3 * (1 << 24):
-        tok_grad, gate_grad, up_grad = pl.pallas_call(
-            functools.partial(gather_kernel, groups, ways, cap),
-            out_shape=(
-                jax.ShapeDtypeStruct((tok_rows, features), BF),
-                jax.ShapeDtypeStruct((block, hidden), F32),
-                jax.ShapeDtypeStruct((block, hidden), F32),
-            ),
-            in_specs=[vmem, vmem, vmem, vmem, hbm, hbm],
+    if groups & (groups - 1) == 0 and bits >= 2 and 8 <= extra and features <= 2048 and held < 9 << 22:
+        far = pl.BlockSpec(memory_space=pltpu.HBM)
+        over = fold_width(extra, features)
+        shapes = (
+            jax.ShapeDtypeStruct((tok_rows, features), BF),
+            jax.ShapeDtypeStruct((block, hidden), F32),
+            jax.ShapeDtypeStruct((block, hidden), F32),
+        )
+        results = pl.pallas_call(
+            functools.partial(gather_kernel, groups, ways, cap, base, extra),
+            out_shape=shapes,
+            in_specs=[far] * 5,
             out_specs=(vmem, vmem, vmem),
             scratch_shapes=[
+                pltpu.VMEM((per_token, tok_rows), jnp.int32),
+                pltpu.VMEM((tok_rows, features), BF),
+                pltpu.VMEM((tok_rows, per_token, hidden), BF),
                 pltpu.VMEM((features, hidden), BF),
                 pltpu.VMEM((features, hidden), BF),
                 pltpu.VMEM((slots, tok_rows), BF),
-                pltpu.VMEM((slots, tok_rows), BF),
-                pltpu.VMEM((slots, tok_rows), BF),
+                pltpu.VMEM((slots, 2 * tok_rows), BF),
+                pltpu.VMEM((2 * tok_rows, hidden), BF),
+                pltpu.VMEM((groups, base, features), BF),
+                pltpu.VMEM((groups, base, hidden), BF),
+                pltpu.VMEM((groups, 16, over + fold_width(extra, hidden)), BF),
                 pltpu.VMEM((groups, cap, features), BF),
                 pltpu.VMEM((groups, cap, hidden), BF),
-                pltpu.VMEM((groups, cap, features), BF),
-                pltpu.VMEM((groups, cap, hidden), BF),
+                pltpu.VMEM((groups, 16, over + fold_width(extra, hidden)), BF),
                 pltpu.VMEM((groups, ways * cap, 2 * hidden), BF),
                 pltpu.VMEM((groups, ways * cap, block), BF),
                 pltpu.VMEM((groups, cap, features), BF),
+                pltpu.VMEM((groups, 16, over), BF),
                 pltpu.VMEM((groups, cap, features), BF),
+                pltpu.VMEM((groups, 16, over), BF),
                 pltpu.VMEM((2, block, hidden), F32),
-                dma((2,)),
-                dma((groups,)),
-                dma((groups,)),
-                dma((groups,)),
-                dma((groups,)),
-                dma((groups,)),
-                dma((groups,)),
-                dma((groups, ways)),
-                dma((groups, ways)),
-                dma((groups, ways, 2)),
-                dma((groups, ways, 2)),
-            ],
-            compiler_params=pltpu.CompilerParams(collective_id=0, has_side_effects=True),
-        )(tokens, routes.T, grad_hidden[:, 0], grad_hidden[:, 1], w_gate[0], w_up[0])
+                dma((5,)),
+            ] + [dma((groups,))] * 10 + [dma((groups, ways))] * 2 + [dma((groups, ways, 2))] * 2,
+            compiler_params=pltpu.CompilerParams(
+                collective_id=0, has_side_effects=True, vmem_limit_bytes=10 << 22),
+        )(pin(routes.T), pin(tokens), pin(grad_hidden), pin(w_gate[0]), pin(w_up[0]))
+        tok_grad, gate_grad, up_grad = pl.pallas_call(
+            flush_kernel,
+            out_shape=shapes,
+            in_specs=[vmem] * 3,
+            out_specs=(far,) * 3,
+            scratch_shapes=[dma((3,))],
+            compiler_params=pltpu.CompilerParams(vmem_limit_bytes=1 << 20),
+        )(*results)
         return tok_grad, gate_grad[None], up_grad[None]
     tok_grad, gate_grad, up_grad = pl.pallas_call(
         functools.partial(kernel, groups, ways, cap),

time: 86.7 us -> 76.3 us (0.88)
  the two profiles are of different devices: /device:TPU:8 before, /device:TPU:0 now
where the time goes in v2:
time: 76.3 us; the launch traced here: 76.1 us
  Pallas kernels  75.5 us (99%)
    pallas_call x1, Pallas kernels, per_device(): pl.pallas_call(functools.partial(gather_kernel, groups, ways, cap, base,...  74.1 us

profile of v2, /device:TPU:0, one launch (start us, length us, event | category | flops | bytes accessed | tf_op | source)
XLA Modules:
  0.0 76.1 jit_solution(17870267838639326771)
XLA Ops:
  0.6 74.1 %shard_map.76 = (bf16[128,2048]{1,0:T(8,128)(2,1)S(1)}, f32[256,768]{1,0:T(8,128)S(1)}, f32[256,768]{1,0:T(8,128)S(1)}) custom-call(s32[2,128]{1,0:T(2,128)} %bitcast.7, bf16[128,2048]{1,0:T(8,128)(2,1)} %tok_hbm.1, bf16[128,2,768]{2,1,0:T(2,128)(2,1)} %gh_hbm.1, bf16[2048,768]{1,0:T(8,128)(2,1)} %bitcast.5, bf16[2048,768]{1,0:T(8,128)(2,1)} %bitcast.6), custom_call_target="tpu_custom_call" | custom-call | tf_op jit(solution)/shard_map/pallas_call | solution.py:569
  74.8 1.3 %shard_map.77 = (bf16[128,2048]{1,0:T(8,128)(2,1)}, f32[256,768]{1,0:T(8,128)}, f32[256,768]{1,0:T(8,128)}) custom-call(bf16[128,2048]{1,0:T(8,128)(2,1)S(1)} %get-tuple-element.9.tok, f32[256,768]{1,0:T(8,128)S(1)} %get-tuple-element.10.gate, f32[256,768]{1,0:T(8,128)S(1)} %get-tuple-element.11.up), custom_call_target="tpu_custom_call" | custom-call | tf_op jit(solution)/shard_map/pallas_call | solution.py:601

commit v3 on v2

--- a/solution.py
+++ b/solution.py
@@ -267,8 +267,8 @@
 def gather_kernel(
     groups, ways, cap, base, extra, rt_hbm, tok_hbm, gh_hbm, wg_hbm, wu_hbm,
     out_tok, out_gate, out_up,
-    rt_ref, tok_ref, gh_ref, wg, wu, pick, both, sides, sx, sd, so, rx, rd, ro, dg, xg, sback, sbo, ret, rbo, acc,
-    l_sem, x_ss, x_rs, d_ss, d_rs, o_ss, o_rs, b_ss, b_rs, e_ss, e_rs, g_ss, g_rs, c_ss, c_rs,
+    rt_ref, tok_ref, gh_ref, wg, wu, pick, both, sides, sx, sd, so, rx, rd, ro, dg, xg, sback, sbo, ret, rbo, tot, acc,
+    l_sem, z_ss, x_rs, d_rs, o_rs, b_rs, e_rs, g_ss, g_rs, c_ss, c_rs,
 ):
     toks, features = tok_ref.shape
     hidden = gh_ref.shape[2]
@@ -276,6 +276,7 @@
     block = features // ways
     bits = ways.bit_length() - 1
     masks, via = gather_plan(bits)
+    passed = sorted({(m ^ (1 << bit), part) for (m, part), bit in via.items()} - {(0, 0), (0, 1)})
     me = lax.axis_index("expert")
     dp = lax.axis_index("dp")
 
@@ -332,19 +333,24 @@
     def rows_of(k, start, count):
         return pl.ds(pl.multiple_of(partner[k] * cap + start, 16), count)
 
-    def to_expert(src, dst, ssem, rsem, k):
+    def to_expert(src, dst, kind, rsem, k):
+        part = pl.ds(0, base if src.shape[1] >= base else src.shape[1])
         return pltpu.make_async_remote_copy(
-            src_ref=src.at[k, pl.ds(0, base)], dst_ref=dst.at[k, pl.ds(0, base)],
-            send_sem=ssem.at[k], recv_sem=rsem.at[k],
+            src_ref=src.at[k, part], dst_ref=dst.at[k, part],
+            send_sem=z_ss.at[kind], recv_sem=rsem.at[k - 1],
             device_id={"expert": partner[k]}, device_id_type=MESH)
 
-    def rest_to_expert(src, dst, ssem, rsem, k):
-        return pltpu.make_async_remote_copy(
-            src_ref=src.at[k], dst_ref=dst.at[k], send_sem=ssem.at[k], recv_sem=rsem.at[k],
-            device_id={"expert": partner[k]}, device_id_type=MESH)
-
-    pending = []
-    x_copy, d_copy, o_copy, b_copy, e_copy = {}, {}, {}, {}, {}
+    def all_sent(ref, sem):
+        pltpu.make_async_remote_copy(
+            src_ref=ref, dst_ref=ref, send_sem=sem, recv_sem=sem,
+            device_id={"dp": peer[1]}, device_id_type=MESH).wait_send()
+
+    def all_got(ref, sem):
+        pltpu.make_async_remote_copy(
+            src_ref=ref, dst_ref=ref, send_sem=sem, recv_sem=sem,
+            device_id={"dp": peer[1]}, device_id_type=MESH).wait_recv()
+
+    x_copy, d_copy, o_copy = {}, {}, {}
     step = 512
     sequence = [0, 1] + list(range(groups - 1, 1, -1))
     load_t.wait()
@@ -358,9 +364,8 @@
             with jax.named_scope("p_barrier"):
                 pl.semaphore_wait(barrier, groups - 1 + ways - 1)
         if k:
-            x_copy[k] = to_expert(sx, rx, x_ss, x_rs, k)
+            x_copy[k] = to_expert(sx, rx, 0, x_rs, k)
             x_copy[k].start()
-            pending.append(x_copy[k])
         if not greeted:
             greeted = True
             load_d.wait()
@@ -369,14 +374,13 @@
         dest = sd if k else rd
         dest[k, 0:count, :] = dot(both[rows_of(k, 0, count), :], sides[...], 1, 0).astype(BF)
         if k:
-            d_copy[k] = to_expert(sd, rd, d_ss, d_rs, k)
+            d_copy[k] = to_expert(sd, rd, 1, d_rs, k)
             d_copy[k].start()
             over = rows_of(k, base, cap - base)
             so[k, :, 0:wide_x] = fold(extra, dot(pick[over, :], tok_ref[...], 1, 0))
             so[k, :, wide_x:] = fold(extra, dot(both[over, :], sides[...], 1, 0))
-            o_copy[k] = rest_to_expert(so, ro, o_ss, o_rs, k)
+            o_copy[k] = to_expert(so, ro, 2, o_rs, k)
             o_copy[k].start()
-            pending += [d_copy[k], o_copy[k]]
 
     tile = 256
 
@@ -391,7 +395,8 @@
         return pltpu.make_async_remote_copy(
             src_ref=dg.at[k, place(mask ^ (1 << bit)), part_cols(part)],
             dst_ref=dg.at[k, place(mask), part_cols(part)],
-            send_sem=c_ss.at[k, mask, part], recv_sem=c_rs.at[k, mask, part],
+            send_sem=c_ss.at[0],
+            recv_sem=c_rs.at[k, passed.index((mask, part)) if (mask, part) in passed else len(passed)],
             device_id={"dp": peer[1 << bit]}, device_id_type=MESH)
 
     def rows_copy(k, mask):
@@ -399,8 +404,17 @@
         return pltpu.make_async_remote_copy(
             src_ref=rx.at[k, :, pl.ds(start, block)],
             dst_ref=xg.at[k, place(mask)],
-            send_sem=g_ss.at[k, mask], recv_sem=g_rs.at[k, mask],
+            send_sem=g_ss.at[0], recv_sem=g_rs.at[k],
             device_id={"dp": peer[mask]}, device_id_type=MESH)
+
+    late = groups >= 4
+    outer = lax.rem(me, 2) == me // (groups // 2)
+    b_copy = {k: to_expert(sback, ret, 3, b_rs, k) for k in sequence[1:]}
+    e_copy = {k: to_expert(sbo, rbo, 4, e_rs, k) for k in sequence[1:]}
+
+    def give_back(k):
+        b_copy[k].start()
+        e_copy[k].start()
 
     waited = set()
 
@@ -414,9 +428,7 @@
         steps.sort(key=lambda step: (via[step] == 0, step[1] != step[0] // (ways // 2)))
         for mask, part in steps:
             arrive(k, mask ^ (1 << via[mask, part]), part)
-            copy = delta_copy(k, mask, part)
-            copy.start()
-            pending.append(copy)
+            delta_copy(k, mask, part).start()
 
     def compute(k):
         if k:
@@ -425,12 +437,14 @@
             with jax.named_scope(f"p_d{k}"):
                 d_copy[k].wait_recv()
                 o_copy[k].wait_recv()
+            if late and k == sequence[-1]:
+                @pl.when(outer)
+                def _():
+                    give_back(sequence[-2])
             rx[k, base:cap, :] = unfold(extra, ro[k, :, 0:wide_x], features)
             rd[k, base:cap, :] = unfold(extra, ro[k, :, wide_x:], hidden)
         for mask in masks[::-1]:
-            copy = rows_copy(k, mask)
-            copy.start()
-            pending.append(copy)
+            rows_copy(k, mask).start()
         if k == 0:
             load_g.wait()
             load_u.wait()
@@ -463,21 +477,23 @@
         with jax.named_scope(f"p_back{k}"):
             lax.fori_loop(0, features // tile, backward, 0)
         if k:
-            b_copy[k] = to_expert(sback, ret, b_ss, b_rs, k)
-            b_copy[k].start()
             sbo[k] = fold(extra, sback[k, base:cap, :].astype(F32))
-            e_copy[k] = rest_to_expert(sbo, rbo, e_ss, e_rs, k)
-            e_copy[k].start()
-            pending.extend([b_copy[k], e_copy[k]])
+            if not late or k != sequence[-2]:
+                give_back(k)
+            if late and k == sequence[-1]:
+                @pl.when(jnp.logical_not(outer))
+                def _():
+                    give_back(sequence[-2])
         start = pl.multiple_of(dp * block, block)
         xg[k, 0:cap, :] = rx[k, :, pl.ds(start, block)]
 
     def weight(k):
         with jax.named_scope(f"p_got{k}"):
-            for mask in masks:
-                rows_copy(k, mask).wait_recv()
-                for part in range(2):
-                    arrive(k, mask, part)
+            all_got(xg.at[k, pl.ds(cap, (ways - 1) * cap)], g_rs.at[k])
+            for mask, part in passed:
+                arrive(k, mask, part)
+            leaves = 2 * (ways - 1) - len(passed)
+            all_got(dg.at[k, pl.ds(0, leaves * cap), part_cols(0)], c_rs.at[k, len(passed)])
         for part in range(2):
             value = dot(xg[k], dg[k, :, part * hidden : (part + 1) * hidden], 0, 0)
             if k == sequence[0]:
@@ -499,22 +515,28 @@
             hop(at + 1 - level, level)
         if bits <= at < groups + bits - 1:
             weight(sequence[at - bits])
-
-    for k in range(1, groups):
+            if at == groups:
+                for c in range(0, features, step):
+                    tot[:, c : c + step] = dot(pick[rows_of(0, 0, cap), :], ret[0, :, c : c + step], 0, 0)
+    weight(sequence[-1])
+
+    for k in sequence[1:]:
         with jax.named_scope(f"p_ret{k}"):
             b_copy[k].wait_recv()
             e_copy[k].wait_recv()
         ret[k, base:cap, :] = unfold(extra, rbo[k], features)
-    for c in range(0, features, step):
-        total = dot(pick[rows_of(0, 0, cap), :], ret[0, :, c : c + step], 0, 0)
-        for k in range(1, groups):
-            total = total + dot(pick[rows_of(k, 0, cap), :], ret[k, :, c : c + step], 0, 0)
-        out_tok[:, c : c + step] = total.astype(BF)
-    weight(sequence[-1])
+        for c in range(0, features, step):
+            total = tot[:, c : c + step] + dot(pick[rows_of(k, 0, cap), :], ret[k, :, c : c + step], 0, 0)
+            if k == sequence[-1]:
+                out_tok[:, c : c + step] = total.astype(BF)
+            else:
+                tot[:, c : c + step] = total
 
     with jax.named_scope("p_drain"):
-        for copy in pending:
-            copy.wait_send()
+        for kind, ref in enumerate((sx, sd, so, sx, sbo)):
+            all_sent(ref.at[pl.ds(1, groups - 1)], z_ss.at[kind])
+        all_sent(xg.at[pl.ds(0, groups), pl.ds(cap, (ways - 1) * cap)], g_ss.at[0])
+        all_sent(dg.at[pl.ds(0, groups), pl.ds(cap, (ways - 1) * cap)], c_ss.at[0])
 
 
 def flush_kernel(tok, gate, up, out_tok, out_gate, out_up, sems):
@@ -592,9 +614,11 @@
                 pltpu.VMEM((groups, 16, over), BF),
                 pltpu.VMEM((groups, cap, features), BF),
                 pltpu.VMEM((groups, 16, over), BF),
+                pltpu.VMEM((tok_rows, features), F32),
                 pltpu.VMEM((2, block, hidden), F32),
                 dma((5,)),
-            ] + [dma((groups,))] * 10 + [dma((groups, ways))] * 2 + [dma((groups, ways, 2))] * 2,
+                dma((5,)),
+            ] + [dma((groups - 1,))] * 5 + [dma((1,)), dma((groups,)), dma((1,)), dma((groups, ways - 1))],
             compiler_params=pltpu.CompilerParams(
                 collective_id=0, has_side_effects=True, vmem_limit_bytes=10 << 22),
         )(pin(routes.T), pin(tokens), pin(grad_hidden), pin(w_gate[0]), pin(w_up[0]))

time: 76.3 us -> 71.4 us (0.936)
  the two profiles are of different devices: /device:TPU:0 before, /device:TPU:8 now
where the time goes in v3:
time: 71.4 us; the launch traced here: 71.3 us
  Pallas kernels  70.6 us (99%)
    pallas_call x1, Pallas kernels, per_device(): pl.pallas_call(functools.partial(gather_kernel, groups, ways, cap, base,...  69.3 us

profile of v3, /device:TPU:8, one launch (start us, length us, event | category | flops | bytes accessed | tf_op | source)
XLA Modules:
  0.0 71.3 jit_solution(11664600787572123513)
XLA Ops:
  0.6 69.3 %shard_map.76 = (bf16[128,2048]{1,0:T(8,128)(2,1)S(1)}, f32[256,768]{1,0:T(8,128)S(1)}, f32[256,768]{1,0:T(8,128)S(1)}) custom-call(s32[2,128]{1,0:T(2,128)} %bitcast.7, bf16[128,2048]{1,0:T(8,128)(2,1)} %tok_hbm.1, bf16[128,2,768]{2,1,0:T(2,128)(2,1)} %gh_hbm.1, bf16[2048,768]{1,0:T(8,128)(2,1)} %bitcast.5, bf16[2048,768]{1,0:T(8,128)(2,1)} %bitcast.6), custom_call_target="tpu_custom_call" | custom-call | tf_op jit(solution)/shard_map/pallas_call | solution.py:591
  69.9 1.3 %shard_map.77 = (bf16[128,2048]{1,0:T(8,128)(2,1)}, f32[256,768]{1,0:T(8,128)}, f32[256,768]{1,0:T(8,128)}) custom-call(bf16[128,2048]{1,0:T(8,128)(2,1)S(1)} %get-tuple-element.9.tok, f32[256,768]{1,0:T(8,128)S(1)} %get-tuple-element.10.gate, f32[256,768]{1,0:T(8,128)S(1)} %get-tuple-element.11.up), custom_call_target="tpu_custom_call" | custom-call | tf_op jit(solution)/shard_map/pallas_call | solution.py:625

commit v4 on v3

--- a/solution.py
+++ b/solution.py
@@ -267,8 +267,8 @@
 def gather_kernel(
     groups, ways, cap, base, extra, rt_hbm, tok_hbm, gh_hbm, wg_hbm, wu_hbm,
     out_tok, out_gate, out_up,
-    rt_ref, tok_ref, gh_ref, wg, wu, pick, both, sides, sx, sd, so, rx, rd, ro, dg, xg, sback, sbo, ret, rbo, tot, acc,
-    l_sem, z_ss, x_rs, d_rs, o_rs, b_rs, e_rs, g_ss, g_rs, c_ss, c_rs,
+    rt_ref, tok_ref, gh_ref, wg, wu, pick, both, sides, sx, sd, so, rx, rd, ro, spos, fpos, far, pfar, rel, dg, xg, sback, sbo, ret, rbo, tot, acc,
+    l_sem, f_ss, f_rs, p_rs, q_rs, z_ss, x_rs, d_rs, o_rs, b_rs, e_rs, g_ss, g_rs, c_ss, c_rs,
 ):
     toks, features = tok_ref.shape
     hidden = gh_ref.shape[2]
@@ -330,6 +330,11 @@
     both[:, 0:toks] = m0.astype(BF)
     both[:, toks:] = m1.astype(BF)
 
+    sub = lax.broadcasted_iota(jnp.int32, (8, toks), 0)
+    spos[...] = jnp.where(sub == 0, pos0, jnp.where(sub == 1, pos1, -1.0))
+    outer = lax.rem(me, 2) == me // (groups // 2)
+    heads = range(2, groups, 2)
+
     def rows_of(k, start, count):
         return pl.ds(pl.multiple_of(partner[k] * cap + start, 16), count)
 
@@ -350,36 +355,73 @@
             src_ref=ref, dst_ref=ref, send_sem=sem, recv_sem=sem,
             device_id={"dp": peer[1]}, device_id_type=MESH).wait_recv()
 
-    x_copy, d_copy, o_copy = {}, {}, {}
+    d_copy, o_copy = {}, {}
     step = 512
-    sequence = [0, 1] + list(range(groups - 1, 1, -1))
+
+    def far_copy(k, c):
+        return pltpu.make_async_remote_copy(
+            src_ref=tok_ref.at[:, pl.ds(c * step, step)], dst_ref=far.at[k // 2 - 1, :, pl.ds(c * step, step)],
+            send_sem=f_ss.at[0], recv_sem=f_rs.at[k // 2 - 1, c],
+            device_id={"expert": partner[k]}, device_id_type=MESH)
+
+    def pos_copy(k):
+        return pltpu.make_async_remote_copy(
+            src_ref=spos, dst_ref=fpos.at[k // 2 - 1], send_sem=f_ss.at[1], recv_sem=p_rs.at[k // 2 - 1],
+            device_id={"expert": partner[k]}, device_id_type=MESH)
+
+    def relay_copy(k, c):
+        cols = pl.ds(c * step, step)
+        return pltpu.make_async_remote_copy(
+            src_ref=rel.at[k // 2 - 1, :, cols], dst_ref=rx.at[k + 1, :, cols],
+            send_sem=f_ss.at[2], recv_sem=q_rs.at[k // 2 - 1],
+            device_id={"expert": partner[1]}, device_id_type=MESH)
+
+    def send_far():
+        for k in heads:
+            for c in range(features // step):
+                far_copy(k, c).start()
+    sequence = list(range(groups))
     load_t.wait()
     greeted = False
-    for k in sequence[1:] + [0]:
-        dest, count = (sx, base) if k else (rx, cap)
-        for c in range(0, features, step):
-            dest[k, 0:count, c : c + step] = dot(
-                pick[rows_of(k, 0, count), :], tok_ref[:, c : c + step], 1, 0).astype(BF)
+    for k in [1, 2] + [1] + sequence[3:] + [0]:
+        count = base if k else cap
+        if k == 0 or not greeted:
+            dest = sx if k else rx
+            for c in range(0, features, step):
+                dest[k, 0:count, c : c + step] = dot(
+                    pick[rows_of(k, 0, count), :], tok_ref[:, c : c + step], 1, 0).astype(BF)
         if not greeted:
             with jax.named_scope("p_barrier"):
                 pl.semaphore_wait(barrier, groups - 1 + ways - 1)
-        if k:
-            x_copy[k] = to_expert(sx, rx, 0, x_rs, k)
-            x_copy[k].start()
+            for far_k in heads:
+                pos_copy(far_k).start()
+            send_far()
         if not greeted:
             greeted = True
+            x_copy = to_expert(sx, rx, 0, x_rs, k)
+            pl.when(jnp.logical_not(outer))(x_copy.start)
             load_d.wait()
             sides[0:toks, :] = gh_ref[:, 0, :]
             sides[toks:, :] = gh_ref[:, 1, :]
+            continue
+        if k == 1:
+            pl.when(outer)(x_copy.start)
         dest = sd if k else rd
         dest[k, 0:count, :] = dot(both[rows_of(k, 0, count), :], sides[...], 1, 0).astype(BF)
         if k:
             d_copy[k] = to_expert(sd, rd, 1, d_rs, k)
             d_copy[k].start()
             over = rows_of(k, base, cap - base)
-            so[k, :, 0:wide_x] = fold(extra, dot(pick[over, :], tok_ref[...], 1, 0))
             so[k, :, wide_x:] = fold(extra, dot(both[over, :], sides[...], 1, 0))
-            o_copy[k] = to_expert(so, ro, 2, o_rs, k)
+            if k == 1:
+                so[k, :, 0:wide_x] = fold(extra, dot(pick[over, :], tok_ref[...], 1, 0))
+                o_copy[k] = to_expert(so, ro, 2, o_rs, k)
+            else:
+                cols = pl.ds(wide_x, so.shape[2] - wide_x)
+                o_copy[k] = pltpu.make_async_remote_copy(
+                    src_ref=so.at[k, :, cols], dst_ref=ro.at[k, :, cols],
+                    send_sem=z_ss.at[5], recv_sem=o_rs.at[k - 1],
+                    device_id={"expert": partner[k]}, device_id_type=MESH)
             o_copy[k].start()
 
     tile = 256
@@ -407,8 +449,6 @@
             send_sem=g_ss.at[0], recv_sem=g_rs.at[k],
             device_id={"dp": peer[mask]}, device_id_type=MESH)
 
-    late = groups >= 4
-    outer = lax.rem(me, 2) == me // (groups // 2)
     b_copy = {k: to_expert(sback, ret, 3, b_rs, k) for k in sequence[1:]}
     e_copy = {k: to_expert(sbo, rbo, 4, e_rs, k) for k in sequence[1:]}
 
@@ -430,21 +470,42 @@
             arrive(k, mask ^ (1 << via[mask, part]), part)
             delta_copy(k, mask, part).start()
 
+    def relay(k):
+        h = k // 2 - 1
+        with jax.named_scope(f"p_pos{k}"):
+            pos_copy(k).wait_recv()
+        slots = lax.broadcasted_iota(jnp.int32, (cap, toks), 0)
+        for which, owner in enumerate((me, partner[1])):
+            here = (slots + owner * cap).astype(F32)
+            pfar[which] = (
+                (here == fpos[h, 0:1, :]).astype(F32) + (here == fpos[h, 1:2, :]).astype(F32)
+            ).astype(BF)
+        for c in range(features // step):
+            with jax.named_scope(f"p_far{k}_{c}"):
+                far_copy(k, c).wait_recv()
+            cols = pl.ds(c * step, step)
+            rel[h, :, cols] = dot(pfar[1], far[h, :, cols], 1, 0).astype(BF)
+            relay_copy(k, c).start()
+            rx[k, :, cols] = dot(pfar[0], far[h, :, cols], 1, 0).astype(BF)
+        for mask in masks[::-1]:
+            rows_copy(k, mask).start()
+
     def compute(k):
         if k:
             with jax.named_scope(f"p_x{k}"):
-                x_copy[k].wait_recv()
+                if k == 1:
+                    x_copy.wait_recv()
+                elif k % 2:
+                    all_got(rx.at[k], q_rs.at[k // 2 - 1])
             with jax.named_scope(f"p_d{k}"):
                 d_copy[k].wait_recv()
                 o_copy[k].wait_recv()
-            if late and k == sequence[-1]:
-                @pl.when(outer)
-                def _():
-                    give_back(sequence[-2])
-            rx[k, base:cap, :] = unfold(extra, ro[k, :, 0:wide_x], features)
+            if k == 1:
+                rx[k, base:cap, :] = unfold(extra, ro[k, :, 0:wide_x], features)
             rd[k, base:cap, :] = unfold(extra, ro[k, :, wide_x:], hidden)
-        for mask in masks[::-1]:
-            rows_copy(k, mask).start()
+        if k < 2 or k % 2:
+            for mask in masks[::-1]:
+                rows_copy(k, mask).start()
         if k == 0:
             load_g.wait()
             load_u.wait()
@@ -478,12 +539,8 @@
             lax.fori_loop(0, features // tile, backward, 0)
         if k:
             sbo[k] = fold(extra, sback[k, base:cap, :].astype(F32))
-            if not late or k != sequence[-2]:
+            if k > 1:
                 give_back(k)
-            if late and k == sequence[-1]:
-                @pl.when(jnp.logical_not(outer))
-                def _():
-                    give_back(sequence[-2])
         start = pl.multiple_of(dp * block, block)
         xg[k, 0:cap, :] = rx[k, :, pl.ds(start, block)]
 
@@ -508,33 +565,91 @@
             with jax.named_scope(f"p_pass{sequence[at]}_{level}"):
                 pass_on(sequence[at], level)
 
-    for at in range(groups + bits):
-        if at < groups:
-            compute(sequence[at])
-        for level in range(2, bits + 1):
-            hop(at + 1 - level, level)
-        if bits <= at < groups + bits - 1:
-            weight(sequence[at - bits])
-            if at == groups:
-                for c in range(0, features, step):
-                    tot[:, c : c + step] = dot(pick[rows_of(0, 0, cap), :], ret[0, :, c : c + step], 0, 0)
-    weight(sequence[-1])
-
-    for k in sequence[1:]:
-        with jax.named_scope(f"p_ret{k}"):
-            b_copy[k].wait_recv()
-            e_copy[k].wait_recv()
-        ret[k, base:cap, :] = unfold(extra, rbo[k], features)
+    compute(0)
+    before = set(waited)
+
+    @pl.when(jnp.logical_not(outer))
+    def _():
+        relay(2)
+        hop(0, 2)
+        compute(2)
+        hop(0, 3)
+        compute(1)
+        give_back(1)
+        hop(2, 2)
+
+    after = set(waited)
+    waited.clear()
+    waited.update(before)
+
+    @pl.when(outer)
+    def _():
+        compute(1)
+        hop(0, 2)
+        relay(2)
+        hop(1, 2)
+        hop(0, 3)
+        compute(2)
+        give_back(1)
+
+    both_ways = after & waited
+    after = after | waited
+    waited.clear()
+    waited.update(both_ways)
+    compute(3)
+    before = set(waited)
+
+    @pl.when(jnp.logical_not(outer))
+    def _():
+        hop(1, 2)
+
+    waited.clear()
+    waited.update(before)
+
+    @pl.when(outer)
+    def _():
+        hop(2, 2)
+
+    waited.update(after)
+
+    def tokens_back(k):
+        if k:
+            with jax.named_scope(f"p_ret{k}"):
+                b_copy[k].wait_recv()
+                e_copy[k].wait_recv()
+            ret[k, base:cap, :] = unfold(extra, rbo[k], features)
         for c in range(0, features, step):
-            total = tot[:, c : c + step] + dot(pick[rows_of(k, 0, cap), :], ret[k, :, c : c + step], 0, 0)
+            total = dot(pick[rows_of(k, 0, cap), :], ret[k, :, c : c + step], 0, 0)
+            if k:
+                total = tot[:, c : c + step] + total
             if k == sequence[-1]:
                 out_tok[:, c : c + step] = total.astype(BF)
             else:
                 tot[:, c : c + step] = total
 
+    hop(1, 3)
+    weight(0)
+    hop(2, 3)
+    tokens_back(0)
+    hop(3, 2)
+    weight(1)
+    hop(3, 3)
+    weight(2)
+    tokens_back(1)
+    tokens_back(2)
+    weight(3)
+    tokens_back(3)
+
     with jax.named_scope("p_drain"):
-        for kind, ref in enumerate((sx, sd, so, sx, sbo)):
-            all_sent(ref.at[pl.ds(1, groups - 1)], z_ss.at[kind])
+        all_sent(sx.at[1], z_ss.at[0])
+        all_sent(so.at[1], z_ss.at[2])
+        for kind, ref in ((1, sd), (3, sback), (4, sbo)):
+            all_sent(ref.at[pl.ds(1, groups - 1), pl.ds(0, min(base, ref.shape[1]))], z_ss.at[kind])
+        all_sent(so.at[pl.ds(2, groups - 2), pl.ds(0, 16), pl.ds(wide_x, so.shape[2] - wide_x)], z_ss.at[5])
+        for _ in heads:
+            all_sent(tok_ref, f_ss.at[0])
+            all_sent(spos, f_ss.at[1])
+        all_sent(rel, f_ss.at[2])
         all_sent(xg.at[pl.ds(0, groups), pl.ds(cap, (ways - 1) * cap)], g_ss.at[0])
         all_sent(dg.at[pl.ds(0, groups), pl.ds(cap, (ways - 1) * cap)], c_ss.at[0])
 
@@ -578,9 +693,9 @@
     extra = max(hot_most, cold_most) - base
     held = 2 * (
         2 * features * hidden + 3 * slots * tok_rows + 5 * slots * (features + hidden)
-        + ways * slots * (2 * hidden + block) + 2 * tok_rows * (features + 4 * hidden)
+        + ways * slots * (2 * hidden + block) + groups * tok_rows * (features + 4 * hidden)
     ) + 4 * 4 * block * hidden
-    if groups & (groups - 1) == 0 and bits >= 2 and 8 <= extra and features <= 2048 and held < 9 << 22:
+    if groups == 4 and bits == 3 and 8 <= extra and features <= 2048 and held < 9 << 22:
         far = pl.BlockSpec(memory_space=pltpu.HBM)
         over = fold_width(extra, features)
         shapes = (
@@ -602,12 +717,17 @@
                 pltpu.VMEM((slots, tok_rows), BF),
                 pltpu.VMEM((slots, 2 * tok_rows), BF),
                 pltpu.VMEM((2 * tok_rows, hidden), BF),
-                pltpu.VMEM((groups, base, features), BF),
+                pltpu.VMEM((2, base, features), BF),
                 pltpu.VMEM((groups, base, hidden), BF),
                 pltpu.VMEM((groups, 16, over + fold_width(extra, hidden)), BF),
                 pltpu.VMEM((groups, cap, features), BF),
                 pltpu.VMEM((groups, cap, hidden), BF),
                 pltpu.VMEM((groups, 16, over + fold_width(extra, hidden)), BF),
+                pltpu.VMEM((8, tok_rows), F32),
+                pltpu.VMEM((groups // 2 - 1, 8, tok_rows), F32),
+                pltpu.VMEM((groups // 2 - 1, tok_rows, features), BF),
+                pltpu.VMEM((2, cap, tok_rows), BF),
+                pltpu.VMEM((groups // 2 - 1, cap, features), BF),
                 pltpu.VMEM((groups, ways * cap, 2 * hidden), BF),
                 pltpu.VMEM((groups, ways * cap, block), BF),
                 pltpu.VMEM((groups, cap, features), BF),
@@ -617,8 +737,13 @@
                 pltpu.VMEM((tok_rows, features), F32),
                 pltpu.VMEM((2, block, hidden), F32),
                 dma((5,)),
-                dma((5,)),
-            ] + [dma((groups - 1,))] * 5 + [dma((1,)), dma((groups,)), dma((1,)), dma((groups, ways - 1))],
+                dma((3,)),
+                dma((groups // 2 - 1, features // 512)),
+                dma((groups // 2 - 1,)),
+                dma((groups // 2 - 1,)),
+                dma((6,)),
+                dma((1,)),
+            ] + [dma((groups - 1,))] * 4 + [dma((1,)), dma((groups,)), dma((1,)), dma((groups, ways - 1))],
             compiler_params=pltpu.CompilerParams(
                 collective_id=0, has_side_effects=True, vmem_limit_bytes=10 << 22),
         )(pin(routes.T), pin(tokens), pin(grad_hidden), pin(w_gate[0]), pin(w_up[0]))

time: 71.4 us -> 69.1 us (0.968)
  the two profiles are of different devices: /device:TPU:8 before, /device:TPU:0 now
where the time goes in v4:
time: 69.1 us; the launch traced here: 68.9 us
  Pallas kernels  68.3 us (99%)
    pallas_call x1, Pallas kernels, per_device(): pl.pallas_call(functools.partial(gather_kernel, groups, ways, cap, base,...  67 us

profile of v4, /device:TPU:0, one launch (start us, length us, event | category | flops | bytes accessed | tf_op | source)
XLA Modules:
  0.0 68.9 jit_solution(13454009158845197592)
XLA Ops:
  0.6 67.0 %shard_map.76 = (bf16[128,2048]{1,0:T(8,128)(2,1)S(1)}, f32[256,768]{1,0:T(8,128)S(1)}, f32[256,768]{1,0:T(8,128)S(1)}) custom-call(s32[2,128]{1,0:T(2,128)} %bitcast.7, bf16[128,2048]{1,0:T(8,128)(2,1)} %tok_hbm.1, bf16[128,2,768]{2,1,0:T(2,128)(2,1)} %gh_hbm.1, bf16[2048,768]{1,0:T(8,128)(2,1)} %bitcast.5, bf16[2048,768]{1,0:T(8,128)(2,1)} %bitcast.6), custom_call_target="tpu_custom_call" | custom-call | tf_op jit(solution)/shard_map/pallas_call | solution.py:706
  67.6 1.3 %shard_map.77 = (bf16[128,2048]{1,0:T(8,128)(2,1)}, f32[256,768]{1,0:T(8,128)}, f32[256,768]{1,0:T(8,128)}) custom-call(bf16[128,2048]{1,0:T(8,128)(2,1)S(1)} %get-tuple-element.9.tok, f32[256,768]{1,0:T(8,128)S(1)} %get-tuple-element.10.gate, f32[256,768]{1,0:T(8,128)S(1)} %get-tuple-element.11.up), custom_call_target="tpu_custom_call" | custom-call | tf_op jit(solution)/shard_map/pallas_call | solution.py:750

commit v5 on v4

--- a/solution.py
+++ b/solution.py
@@ -627,11 +627,11 @@
             else:
                 tot[:, c : c + step] = total
 
+    hop(3, 2)
     hop(1, 3)
+    hop(2, 3)
     weight(0)
-    hop(2, 3)
     tokens_back(0)
-    hop(3, 2)
     weight(1)
     hop(3, 3)
     weight(2)

time: 69.1 us -> 67.4 us (0.975)
  the two profiles are of different devices: /device:TPU:0 before, /device:TPU:8 now
where the time goes in v5:
time: 67.4 us; the launch traced here: 66.3 us
  Pallas kernels  65.6 us (97%)
    pallas_call x1, Pallas kernels, per_device(): pl.pallas_call(functools.partial(gather_kernel, groups, ways, cap, base,...  64.3 us

profile of v5, /device:TPU:8, one launch (start us, length us, event | category | flops | bytes accessed | tf_op | source)
XLA Modules:
  0.0 66.3 jit_solution(7455182394875698890)
XLA Ops:
  0.6 64.3 %shard_map.76 = (bf16[128,2048]{1,0:T(8,128)(2,1)S(1)}, f32[256,768]{1,0:T(8,128)S(1)}, f32[256,768]{1,0:T(8,128)S(1)}) custom-call(s32[2,128]{1,0:T(2,128)} %bitcast.7, bf16[128,2048]{1,0:T(8,128)(2,1)} %tok_hbm.1, bf16[128,2,768]{2,1,0:T(2,128)(2,1)} %gh_hbm.1, bf16[2048,768]{1,0:T(8,128)(2,1)} %bitcast.5, bf16[2048,768]{1,0:T(8,128)(2,1)} %bitcast.6), custom_call_target="tpu_custom_call" | custom-call | tf_op jit(solution)/shard_map/pallas_call | solution.py:706
  64.9 1.3 %shard_map.77 = (bf16[128,2048]{1,0:T(8,128)(2,1)}, f32[256,768]{1,0:T(8,128)}, f32[256,768]{1,0:T(8,128)}) custom-call(bf16[128,2048]{1,0:T(8,128)(2,1)S(1)} %get-tuple-element.9.tok, f32[256,768]{1,0:T(8,128)S(1)} %get-tuple-element.10.gate, f32[256,768]{1,0:T(8,128)S(1)} %get-tuple-element.11.up), custom_call_target="tpu_custom_call" | custom-call | tf_op jit(solution)/shard_map/pallas_call | solution.py:750
